TPU v7x, 128 devices: a whole 4x4x4 slice. The times are simulated.
128 devices in a mesh: row: 8 (over z, y_hi), col: 16 (over x, y_lo, core).
Axes of the slice: x: 4, y: 4 (y_hi: 2, y_lo: 2; y = y_hi * 2 + y_lo), z: 4, core: 2. Of those that a mesh axis runs over, the one named last changes fastest.
Arguments:
- tokens_in: bfloat16 [16384, 1408], P(('row', 'col')), may hold values from -300 to 300
- ln1_gain: bfloat16 [1408], replicated, may hold values from 0.099609375 to 1.8984375
- ln1_bias: bfloat16 [1408], replicated, may hold values from -3 to 3
- qkv_weight: bfloat16 [1408, 4224], P('row', 'col'), may hold values from -0.8 to 0.8
- qkv_bias: bfloat16 [4224], P('col'), may hold values from -3 to 3
- proj_weight: bfloat16 [1408, 1408], P('col', 'row'), may hold values from -0.15625 to 0.15625
- proj_bias: bfloat16 [1408], replicated, may hold values from -3 to 3
- ln2_gain: bfloat16 [1408], replicated, may hold values from 0.099609375 to 1.8984375
- ln2_bias: bfloat16 [1408], replicated, may hold values from -3 to 3
- fc1_weight: bfloat16 [1408, 6144], P('row', 'col'), may hold values from -0.15625 to 0.15625
- fc1_bias: bfloat16 [6144], P('col'), may hold values from -3 to 3
- fc2_weight: bfloat16 [1408, 6144], P('row', 'col'), may hold values from -0.078125 to 0.078125
- fc2_bias: bfloat16 [1408], replicated, may hold values from -3 to 3
Outputs:
- tokens_out: bfloat16 [16384, 1408], P(('row', 'col'))
All inputs are finite; a program needn't handle non-finite values.
Results may differ from a plain program's by a relative error of at most 0.01.
Values may be sent and summed in bfloat16 or wider, within the bound.
A program may use at most 64 MiB of HBM per device.

v0:
```python
import jax
import jax.numpy as jnp
from jax import lax
from jax.experimental import pallas as pl
from jax.experimental.pallas import tpu as pltpu
from jax.sharding import PartitionSpec as P

MESH = pl.DeviceIdType.MESH
F32 = jnp.float32
BF16 = jnp.bfloat16
D = 1408
HEAD = 88
COPIES = 122
SENDS = 28
FR = 80
YZ, ZY = "yz", "zy"
FIRST, SECOND = ZY, YZ
PM, IO = "pm", "io"
ORDER = (
    18, 74, 54, 73, 39, 3, 40, 55, 16, 1, 2, 0, 20, 14, 41, 56, 91, 22, 27, 19, 5, 45, 17, 75, 57,
    44, 4, 89, 21, 24, 13, 23, 42, 47, 59, 15, 29, 9, 8, 6, 43, 7, 58, 28, 77, 31, 46, 25, 62, 34,
    35, 32, 30, 26, 10, 88, 11, 60, 61, 68, 12, 33, 48, 80, 67, 49, 51, 50, 64, 65, 79, 104, 71,
    103, 36, 106, 37, 98, 85, 107, 86, 97, 38, 69, 70, 105, 83, 108, 63, 109, 53, 110, 52, 113, 114,
    119, 120, 72, 95, 111, 112, 90, 123, 124, 66, 115, 116, 121, 81, 122, 117, 118, 99, 82, 94, 87,
    76, 100, 93, 101, 92, 125, 126, 127, 84, 128, 133, 139, 130, 96, 78, 136, 102, 140, 134, 131,
    145, 137, 141, 142, 132, 135, 138, 129, 148, 153, 152, 147, 144, 158, 163, 162, 150, 156, 143,
    146, 160, 173, 164, 167, 170, 149, 155, 154, 159, 165, 166, 174, 175, 168, 169, 171, 172, 151,
    157, 161, 176,
)
SLOTS = (
    0, 1, 2, 3, 4, 5, 6, 7, 8, 9, 10, 11, 12, 13, 14, 15, 16, 17, 18, 4, 2, 6, 19, 20, 21, 22, 5, 0,
    7, 8, 14, 1, 3, 10, 12, 13, 15, 2, 9, 11, 23, 24, 25, 4, 26, 21, 6, 5, 18, 7, 17, 16, 20, 3, 0,
    22, 19, 8, 14, 10, 12, 1, 13, 9, 25, 7, 11, 2, 26, 17, 27, 23, 16, 24, 6, 15, 4, 12, 21, 1, 0,
    18, 8, 19, 14, 3, 5, 10, 9, 20, 25, 16, 24, 17, 11, 13, 26, 21, 22, 23, 4, 12, 27, 2, 7, 6, 0,
    18, 15, 1, 19, 14, 8, 25, 3, 5, 10, 24, 16, 17, 20, 11, 26, 13, 9, 22, 23, 4, 21, 0, 12, 27, 7,
    18, 2, 15, 1, 6, 8, 19, 25, 14, 10, 5, 16, 11,
)
SCALE = (1.0 / HEAD**0.5) * 1.4426950408889634
NT = (((1,), (1,)), ((), ()))


def norm(values, gain, bias):
    mean = jnp.mean(values, axis=-1, keepdims=True)
    centred = values - mean
    var = jnp.mean(centred * centred, axis=-1, keepdims=True)
    return centred * lax.rsqrt(var + 1e-06) * gain + bias


class Names:
    def __getattr__(self, name):
        return name


def panel(w):
    lane = lax.broadcasted_iota(jnp.int32, (w.shape[0], 128), 1)
    rest = jnp.concatenate([w[:, 176:264], jnp.zeros((w.shape[0], 40), F32)], axis=1)
    parts = [w[:, 0:128], w[:, 88:216], rest]
    return [jnp.where(lane < HEAD, part, 0.0) for part in parts]


def kernel(
    tok_in, g1, b1, pb, g2, b2, cb, qb, fb, wq, wp, f1, f2, out,
    X, WQ, QB, WP, F1, F2, FB, QKV, O, OA, PP, PS, PR, RES, H, PART, SS, SD, KEEP, DS, RS_R, RS_L,
    RA, RB, RL, RR, tok, QR, WR, WT, v0, v1, v2, v3, v4, v5, vq, vf,
    send, recv, lsem,
):
    r = lax.axis_index("row")
    c = lax.axis_index("col")
    z, yh = r // 2, r % 2
    x, yl, core = c // 4, (c // 2) % 2, c % 2
    y = yh * 2 + yl
    chip = c // 2

    def plus(v, n):
        return lax.rem(v + n, 4)

    def at_x(v):
        return (r, v * 4 + yl * 2 + core)

    def at_y(v):
        return (z * 2 + v // 2, x * 4 + lax.rem(v, 2) * 2 + core)

    def at_z(v):
        return (v * 2 + yh, c)

    left, right, far = plus(x, 3), plus(x, 1), plus(x, 2)
    zb, zf, z2 = plus(z, 3), plus(z, 1), plus(z, 2)
    yi, yo, y2 = yh * 2 + 1 - yl, plus(y, 3 + 2 * yl), plus(y, 2)
    xs = {"p": at_x(right), "m": at_x(left)}
    ys = {"i": at_y(yi), "o": at_y(yo)}
    zs = {"p": at_z(zf), "m": at_z(zb)}
    dd = (r, x * 4 + yl * 2 + 1 - core)

    barrier = pltpu.get_barrier_semaphore()
    peers = [*xs.values(), *ys.values(), *zs.values(), dd]
    for peer in peers:
        pl.semaphore_signal(barrier, inc=1, device_id=peer, device_id_type=MESH)

    def cols(yv):
        return pl.ds(pl.multiple_of(lax.rem(yv, 2) * 384, 384), 384)

    def lanes(xv, yv):
        return pl.ds(pl.multiple_of(lax.rem(yv, 2) * 512 + xv * 128, 128), 128)

    def line(yv):
        return pl.ds(pl.multiple_of(lax.rem(yv, 2) * 512, 512), 512)

    def piece(F, zv, yv):
        return F.at[zv, yv // 2, :, cols(yv)]

    pairs = [
        (tok_in, tok), (g1, v0), (b1, v1), (wq, QR), (wp, WR), (qb, vq), (pb, v2), (g2, v3),
        (b2, v4), (cb, v5), (fb, vf), (f2, piece(F2, z, y)), (f1, piece(F1, z, y)),
    ]
    loads = [pltpu.make_async_copy(src, dst, lsem.at[i]) for i, (src, dst) in enumerate(pairs)]
    for load in loads:
        load.start()

    def row(ref):
        return ref[...].astype(F32).reshape(1, -1)

    with jax.named_scope("prep"):
        for load in loads[:11]:
            load.wait()
        inputs = tok[...].astype(F32)
        X[chip, core] = norm(inputs, row(v0), row(v1)).astype(BF16)
        for i, part in enumerate(panel(QR[...].astype(F32))):
            WQ[z, yh, :, i * 128 : (i + 1) * 128] = part.astype(BF16)
        WT[...] = jnp.zeros((128, 256), F32)
        WT[0:HEAD, 0:176] = WR[...].astype(F32)
        WP[z, yh, :, lanes(x, yl)] = WT[...].T[0:176].astype(BF16)
        FB[yl] = jnp.broadcast_to(row(vf), (8, 384))
        for load in loads[11:]:
            load.wait()
    with jax.named_scope("w_barrier"):
        pl.semaphore_wait(barrier, len(peers))

    t = Names()
    acts = {}

    def push(name, deps, ref, dev):
        acts[name] = (deps, ref, ref, dev)

    def go(name, deps, src, dst, dev):
        acts[name] = (deps, src, dst, dev)

    def calc(name, deps, step):
        acts[name] = (deps, step)

    top, low = pl.ds(0, 64), pl.ds(64, 64)
    ra, rb = pl.ds(0, 96), pl.ds(96, 80)

    def blk(xv, yv, rows=None):
        where = xv * 2 + lax.rem(yv, 2)
        return X.at[where, core] if rows is None else X.at[where, core, rows]

    push(t.qzp, [], WQ.at[z, yh], zs[t.p])
    push(t.qzm, [], WQ.at[z, yh], zs[t.m])
    go(t.qr1, [], WQ.at[z, yh, ra], QB.at[ra], ys[t.i])
    go(t.qr2, [], WQ.at[z, yh, rb], QB.at[rb], ys[t.i])
    go(t.qf1, [t.qr1], QB.at[ra], WQ.at[z, yh, ra], ys[t.o])
    go(t.qf2, [t.qr2], QB.at[rb], WQ.at[z, yh, rb], ys[t.o])
    push(t.qzfp, [t.qzp], WQ.at[zb, yh, ra], zs[t.p])
    push(t.qzfm, [t.qzm], WQ.at[zf, yh, rb], zs[t.m])
    for d in PM:
        push(t.q2z + d, [t.qf1, t.qf2], WQ.at[z, 1 - yh], zs[d])
    push(t.q2zfp, [t.q2zp], WQ.at[zb, 1 - yh, ra], zs[t.p])
    push(t.q2zfm, [t.q2zm], WQ.at[zf, 1 - yh, rb], zs[t.m])

    push(t.ad, [], blk(x, yl), dd)
    push(t.by, [], FB.at[yl], ys[t.i])
    near = {t.p: (left, top, low), t.m: (right, low, top)}
    quarter = {t.p: (t.a, pl.ds(0, 32), t.b, pl.ds(32, 32)), t.m: (t.a, pl.ds(64, 32), t.b, pl.ds(96, 32))}
    quarters = [
        (d, near[d][0], e, rows) for d, (e1, r1, e2, r2) in quarter.items() for e, rows in ((e1, r1), (e2, r2))
    ]
    for d, side, e, rows in quarters:
        push(t.a1 + e + d, [], blk(x, yl, rows), xs[d])
        push(t.af + e + d, [t.a1 + e + d], blk(side, yl, rows), xs[d])
    for d, (side, first, second) in near.items():
        push(t.a2 + d, [], blk(x, yl, second), xs[d])
    for k, rows in (("1", top), ("2", low)):
        push(t.ay + k, [], blk(x, yl, rows), ys[t.i])
        for d in PM:
            push(t.yx + k + d, [t.ay + k], blk(x, 1 - yl, rows), xs[d])
    push(t.d2y1, [t.afap, t.afbp], blk(far, yl, top), ys[t.i])
    push(t.d2y2, [t.afam, t.afbm], blk(far, yl, low), ys[t.i])
    push(t.ld, [t.a1ap, t.a1bp, t.a2p], blk(left, yl), dd)
    push(t.rd, [t.a1am, t.a1bm, t.a2m], blk(right, yl), dd)
    push(t.p0d, [t.ay1, t.ay2], blk(x, 1 - yl), dd)
    push(t.d2d, [t.afap, t.afbp, t.afam, t.afbm], blk(far, yl), dd)
    push(t.pld, [t.yx1p, t.yx2p], blk(left, 1 - yl), dd)
    push(t.prd, [t.yx1m, t.yx2m], blk(right, 1 - yl), dd)
    push(t.pd2d, [t.d2y1, t.d2y2], blk(far, 1 - yl), dd)

    ua, ub = pl.ds(0, FR), pl.ds(FR, 176 - FR)
    for d in IO:
        push(t.wa + d, [], WP.at[z, yh, ua, lanes(x, yl)], ys[d])
    push(t.waf, [t.wai], WP.at[z, yi // 2, ua, lanes(x, yi)], ys[t.o])
    waz = [t.wazfp, t.wazfm]
    for d in PM:
        for v in (0, 1):
            waz.append(t.waz + str(v) + d)
            push(waz[-1], [t.wai, t.wao, t.waf], WP.at[z, :, ua, lanes(x, v)], zs[d])
    push(t.wazfp, [t.waz0p], WP.at[zb, :, ua, lanes(x, 0)], zs[t.p])
    push(t.wazfm, [t.waz1m], WP.at[zf, :, ua, lanes(x, 1)], zs[t.m])
    whole = [t.waxfp, t.waxfm]
    for d in PM:
        for v in (0, 1):
            whole.append(t.wax + str(v) + d)
            push(whole[-1], waz, WP.at[:, :, ua, lanes(x, v)], xs[d])
    push(t.waxfp, [t.wax0p], WP.at[:, :, ua, lanes(left, 0)], xs[t.p])
    push(t.waxfm, [t.wax1m], WP.at[:, :, ua, lanes(right, 1)], xs[t.m])
    wide = (176 - FR) // 2
    push(t.wbxp, [], WP.at[z, yh, ub, lanes(x, yl)], xs[t.p])
    push(t.wbxm, [], WP.at[z, yh, ub, lanes(x, yl)], xs[t.m])
    push(t.wbxfp, [t.wbxp], WP.at[z, yh, pl.ds(FR, wide), lanes(left, yl)], xs[t.p])
    push(t.wbxfm, [t.wbxm], WP.at[z, yh, pl.ds(FR + wide, wide), lanes(right, yl)], xs[t.m])
    wbx = [t.wbxp, t.wbxm, t.wbxfp, t.wbxfm]

    def wline(zv, yv):
        return WP.at[zv, yv // 2, ub, line(yv)]

    push(t.wbyi, wbx, wline(z, y), ys[t.i])
    push(t.wbyo, wbx, wline(z, y), ys[t.o])
    push(t.wbyf, [t.wbyi], wline(z, yi), ys[t.o])
    for j, (yv, deps) in enumerate(((y, wbx), (yi, [t.wbyi]), (yo, [t.wbyo]), (y2, [t.wbyf]))):
        name = t.wbz + str(j)
        push(name + t.p, deps, wline(z, yv), zs[t.p])
        push(name + t.m, deps, wline(z, yv), zs[t.m])
        d, zv = (t.p, zb) if j < 2 else (t.m, zf)
        push(t.wbzf + str(j), [name + d], wline(zv, yv), zs[d])
        whole += [name + t.p, name + t.m, t.wbzf + str(j)]

    panels = [t.by]

    def spread(n, F, order, flip):
        if order == YZ:
            push(n + t.yi, [], piece(F, z, y), ys[t.i])
            push(n + t.yo, [], piece(F, z, y), ys[t.o])
            push(n + t.yf, [n + t.yi], piece(F, z, yi), ys[t.o])
            panels.extend([n + t.yi, n + t.yo, n + t.yf])
            parts = ((y, []), (yi, [n + t.yi]), (yo, [n + t.yo]), (y2, [n + t.yf]))
            for j, (yv, deps) in enumerate(parts):
                name = n + t.z + str(j)
                push(name + t.p, deps, piece(F, z, yv), zs[t.p])
                push(name + t.m, deps, piece(F, z, yv), zs[t.m])
                d, zv = (t.p, zb) if j < 2 else (t.m, zf)
                push(n + t.zf + str(j), [name + d], piece(F, zv, yv), zs[d])
                panels.extend([name + t.p, name + t.m, n + t.zf + str(j)])
        else:
            push(n + t.zp, [], piece(F, z, y), zs[t.p])
            push(n + t.zm, [], piece(F, z, y), zs[t.m])
            d, zv = (t.m, zf) if flip else (t.p, zb)
            push(n + t.zf, [n + t.z + d], piece(F, zv, y), zs[d])
            panels.extend([n + t.zp, n + t.zm, n + t.zf])
            parts = ((z, []), (zb, [n + t.zp]), (zf, [n + t.zm]), (z2, [n + t.zf]))
            for j, (zv, deps) in enumerate(parts):
                push(n + t.yi + str(j), deps, piece(F, zv, y), ys[t.i])
                push(n + t.yo + str(j), deps, piece(F, zv, y), ys[t.o])
                push(n + t.yf + str(j), [n + t.yi + str(j)], piece(F, zv, yi), ys[t.o])
                panels.extend([n + t.yi + str(j), n + t.yo + str(j), n + t.yf + str(j)])

    spread(t.f1, F1, FIRST, True)
    spread(t.f2, F2, SECOND, False)

    bias = jnp.concatenate(panel(row(vq)), axis=1)
    ones = lax.broadcasted_iota(jnp.int32, (1, 384), 1) == 256 + HEAD
    bias = jnp.where(ones, 1.0, bias)

    spots = [
        (x, yl), (left, yl), (right, yl), (x, 1 - yl), (far, yl),
        (left, 1 - yl), (right, 1 - yl), (far, 1 - yl),
    ]

    def qkv(j):
        def step():
            xv, yv = spots[j]
            h = X[xv * 2 + lax.rem(yv, 2)].reshape(256, D)
            product = jnp.dot(h, WQ[...].reshape(D, 384), preferred_element_type=F32)
            QKV[j] = (product + bias).astype(BF16)

        return step

    weights = [
        t.qzp, t.qzm, t.qf1, t.qf2, t.qzfp, t.qzfm, t.q2zp, t.q2zm, t.q2zfp, t.q2zfm,
    ]
    calc(t.k0, weights + [t.ad], qkv(0))
    calc(t.k1, weights + [t.ld, t.a1ap, t.a1bp, t.a2p], qkv(1))
    calc(t.k2, weights + [t.rd, t.a1am, t.a1bm, t.a2m], qkv(2))
    calc(t.k3, weights + [t.p0d, t.ay1, t.ay2], qkv(3))
    calc(t.k4, weights + [t.d2d, t.afap, t.afbp, t.afam, t.afbm], qkv(4))
    calc(t.k5, weights + [t.pld, t.yx1p, t.yx2p], qkv(5))
    calc(t.k6, weights + [t.prd, t.yx1m, t.yx2m], qkv(6))
    calc(t.k7, weights + [t.pd2d, t.d2y1, t.d2y2], qkv(7))

    slot = lanes(x, yl)

    def attend(j):
        def step():
            keys = QKV[:, :, 128:256].reshape(2048, 128)
            values = QKV[:, :, 256:384].reshape(2048, 128)

            def scores(i):
                q = QKV[j, i * 128 : i * 128 + 128, 0:128]
                return lax.dot_general(q, keys, NT, preferred_element_type=F32)

            def mix(i, s):
                most = jnp.max(s, axis=-1, keepdims=True)
                p = jnp.exp2((s - most) * SCALE).astype(BF16)
                mixed = jnp.dot(p, values, preferred_element_type=F32)
                o = (mixed / mixed[:, HEAD : HEAD + 1]).astype(BF16)
                if j == 0:
                    OA[i, :, slot] = o
                else:
                    O[j, i] = o

            first, second = scores(0), scores(1)
            mix(0, first)
            mix(1, second)

        return step

    every = [t.k + str(i) for i in range(8)]
    homes = []
    for i, j in enumerate((7, 4, 5, 1, 6, 2, 3, 0)):
        calc(t.at + str(i), every, attend(j))
        if j:
            xv, yv = spots[j]
            whose = (r, (xv * 2 + lax.rem(yv, 2)) * 2 + core)
            go(t.o + str(i), [t.at + str(i)], O.at[j], OA.at[:, :, slot], whose)
            homes.append(t.o + str(i))

    def project():
        heads = OA[...].reshape(256, 1024)
        part = lax.dot_general(heads, WP[...].reshape(D, 1024), NT, preferred_element_type=F32)
        PP[...] = part.reshape(2, 128, D)
        PS[...] = PP[1 - core].astype(BF16)

    calc(t.pr, whole + homes + [t.at + str(i) for i in range(8)], project)
    go(t.ps, [t.pr], PS, PR, dd)

    def second_norm():
        resid = tok[...].astype(F32) + PP[core] + PR[...].astype(F32) + row(v2)
        RES[...] = resid
        H[x, core] = norm(resid, row(v3), row(v4)).astype(BF16)

    calc(t.ln, [t.pr, t.ps], second_norm)

    push(t.hd, [t.ln], H.at[x, core], dd)
    for d, side, e, rows in quarters:
        push(t.h1 + e + d, [t.ln], H.at[x, core, rows], xs[d])
        push(t.hf + e + d, [t.h1 + e + d], H.at[side, core, rows], xs[d])
        other = t.m if d == t.p else t.p
        push(t.h2 + e + other, [t.ln], H.at[x, core, rows], xs[other])
    for d, (side, first, second) in near.items():
        push(t.hd1 + d, [t.h1 + t.a + d, t.h1 + t.b + d], H.at[side, core, first], dd)
        push(t.hd2 + d, [t.h2 + t.a + d, t.h2 + t.b + d], H.at[side, core, second], dd)
        push(t.hfd + d, [t.hf + t.a + d, t.hf + t.b + d], H.at[far, core, first], dd)

    def rows_of(v):
        return slice(v * 64, v * 64 + 64)

    def mlp(*parts):
        def step():
            h = [H[where, :, rows_of(v), :].reshape(128, D) for _, where, v in parts]
            h = jnp.concatenate(h, axis=0)
            a = jnp.dot(h, F1[...].reshape(D, 768), preferred_element_type=F32)
            a = a + jnp.concatenate([FB[0, 0:1, :], FB[1, 0:1, :]], axis=1)
            hidden = (0.5 * a * (1.0 + lax.erf(a * 0.7071067811865476))).astype(BF16)
            part = lax.dot_general(hidden, F2[...].reshape(D, 768), NT, preferred_element_type=F32)
            for i, (k, _, v) in enumerate(parts):
                PART[k, :, rows_of(v), :] = part[i * 128 : i * 128 + 128].reshape(2, 64, D)
                SS[k, rows_of(v), :] = PART[k, 1 - core, rows_of(v), :].astype(BF16)

        return step

    arrived_1 = [t.hd1p, t.hd1m, t.h1ap, t.h1bp, t.h1am, t.h1bm]
    arrived_2 = [t.hd2p, t.hd2m, t.h2ap, t.h2bp, t.h2am, t.h2bm]
    arrived_f = [t.hfdp, t.hfdm, t.hfap, t.hfbp, t.hfam, t.hfbm]
    calc(t.mA, panels + arrived_1, mlp((1, left, 0), (2, right, 1)))
    calc(t.mB, panels + arrived_2, mlp((1, left, 1), (2, right, 0)))
    calc(t.mF, panels + arrived_f, mlp((3, far, 0), (3, far, 1)))
    calc(t.mo, panels + [t.ln, t.hd], mlp((0, x, 0), (0, x, 1)))
    go(t.sAp, [t.mA], SS.at[1, top], SD.at[1, top], dd)
    go(t.sAm, [t.mA], SS.at[2, low], SD.at[2, low], dd)
    go(t.sBp, [t.mB], SS.at[1, low], SD.at[1, low], dd)
    go(t.sBm, [t.mB], SS.at[2, top], SD.at[2, top], dd)
    go(t.sF, [t.mF], SS.at[3], SD.at[3], dd)
    go(t.so, [t.mo], SS.at[0], SD.at[0], dd)

    def total(k, v=None):
        rows = slice(0, 128) if v is None else rows_of(v)
        return PART[k, core, rows, :] + SD[k, rows, :].astype(F32)

    def sum_first():
        RS_L[0:64] = total(1, 0).astype(BF16)
        RS_R[64:128] = total(2, 1).astype(BF16)

    def sum_second():
        KEEP[1] = total(1, 1)
        KEEP[0] = total(2, 0)

    def sum_far():
        DS[...] = total(3).astype(BF16)

    def sum_own():
        RES[...] = RES[...] + total(0) + row(v5)

    def add(mine, kept, came, lo):
        def step():
            rows = slice(lo % 64, lo % 64 + 32)
            mine[lo : lo + 32] = (KEEP[kept, rows, :] + came[rows].astype(F32)).astype(BF16)

        return step

    def finish():
        out[...] = (RES[...] + RL[...].astype(F32) + RR[...].astype(F32)).astype(BF16)

    calc(t.cA, [t.mA, t.sAp, t.sAm], sum_first)
    calc(t.cB, [t.mB, t.sBp, t.sBm], sum_second)
    calc(t.cF, [t.mF, t.sF], sum_far)
    calc(t.co, [t.mo, t.so, t.ln], sum_own)
    go(t.ma, [t.cA], RS_L.at[top], RR.at[top], xs[t.m])
    go(t.pb, [t.cA], RS_R.at[low], RL.at[low], xs[t.p])
    last = [t.co, t.ma, t.pb]
    for d, side, e, rows in quarters:
        lo = (0 if d == t.p else 64) + (0 if e == t.a else 32)
        came, mine, kept, dest = (RA, RS_R, 0, RL) if d == t.p else (RB, RS_L, 1, RR)
        go(t.da + e + d, [t.cF], DS.at[rows], came.at[pl.ds(lo % 64, 32)], xs[d])
        calc(t.e + e + d, [t.cB, t.da + e + d], add(mine, kept, came, lo))
        go(t.p + e + d, [t.e + e + d], mine.at[rows], dest.at[rows], xs[d])
        last.append(t.p + e + d)
    calc(t.end, last, finish)

    names = list(acts)
    moves = [name for name in names if len(acts[name]) == 4]
    passed_on = {dep for name in moves for dep in acts[name][0]}

    def finals(prefix):
        return [name for name in moves if name.startswith(prefix) and name not in passed_on]

    groups = [
        (homes, O.at[pl.ds(1, 7)]),
        (finals(t.f1), F1.at[pl.ds(0, 2)]),
        (finals(t.f2), F2.at[pl.ds(0, 2)]),
        (finals(t.wbz), WP.at[pl.ds(0, 2), :, ub, :]),
        (finals(t.wax), WP.at[:, :, ua, pl.ds(0, 512)]),
    ]
    assert [len(members) for members, _ in groups] == [7, 8, 8, 8, 4]
    group_of = {name: g for g, (members, _) in enumerate(groups) for name in members}
    early = [name for name in moves if name[0] in t.aq or name in (t.ld, t.rd, t.p0d, t.pld, t.prd)]
    early += [name for name in moves if name[:2] == t.yx or name[:2] == t.d2 or name == t.pd2d]
    late = moves[moves.index(t.hd):]
    slots = {name: i for i, name in enumerate(early)}
    slots.update(zip(late, range(len(late))))
    count = len(early)
    for name in moves:
        if name not in slots:
            if name in group_of:
                for member in groups[group_of[name]][0]:
                    slots[member] = count
            else:
                slots[name] = count
            count += 1
    assert len(early) >= len(late) and count <= COPIES

    done, sent, arrived, busy = set(), {}, set(), {}

    def expect(dep):
        if dep in arrived:
            return
        with jax.named_scope("w_" + dep):
            if dep in group_of:
                members, ref = groups[group_of[dep]]
                pltpu.make_async_remote_copy(
                    src_ref=ref, dst_ref=ref, send_sem=send.at[0], recv_sem=recv.at[slots[dep]],
                    device_id=dd, device_id_type=MESH,
                ).wait_recv()
                arrived.update(members)
            else:
                sent[dep].wait_recv()
                arrived.add(dep)

    turn = 0
    for number in ORDER:
        name = names[number]
        deps = acts[name][0]
        for dep in deps:
            assert dep in done
            if dep in sent:
                expect(dep)
        if len(acts[name]) == 2:
            with jax.named_scope("c_" + name):
                acts[name][1]()
        else:
            _, src, dst, dev = acts[name]
            i = SLOTS[turn]
            turn += 1
            if i in busy:
                with jax.named_scope("s_" + busy[i]):
                    sent[busy[i]].wait_send()
            busy[i] = name
            sent[name] = pltpu.make_async_remote_copy(
                src_ref=src, dst_ref=dst, send_sem=send.at[i], recv_sem=recv.at[slots[name]],
                device_id=dev, device_id_type=MESH,
            )
            sent[name].start()
        done.add(name)
    assert len(done) == len(acts)
    for name in moves:
        expect(name)
    for name in busy.values():
        sent[name].wait_send()


def local(
    tokens_in, ln1_gain, ln1_bias, qkv_weight, qkv_bias, proj_weight, proj_bias,
    ln2_gain, ln2_bias, fc1_weight, fc1_bias, fc2_weight, fc2_bias,
):
    vmem = pl.BlockSpec(memory_space=pltpu.VMEM)
    hbm = pl.BlockSpec(memory_space=pltpu.HBM)
    dma = pltpu.SemaphoreType.DMA
    def big(*shape):
        return pltpu.VMEM(shape, BF16)

    scratch = [
        big(8, 2, 128, D), big(4, 2, 176, 384), big(176, 384), big(4, 2, 176, 1024),
        big(4, 2, 176, 768), big(4, 2, 176, 768), pltpu.VMEM((2, 8, 384), F32),
        big(8, 256, 384), big(8, 2, 128, 128), big(2, 128, 1024), pltpu.VMEM((2, 128, D), F32),

        big(128, D), big(128, D), pltpu.VMEM((128, D), F32), big(4, 2, 128, D),
        pltpu.VMEM((4, 2, 128, D), F32), big(4, 128, D), big(4, 128, D), pltpu.VMEM((2, 64, D), F32),
        big(128, D), big(128, D), big(128, D), big(64, D), big(64, D), big(128, D), big(128, D),
        big(128, D), big(176, 264), big(HEAD, 176), pltpu.VMEM((128, 256), F32),
        *[big(n) for n in (D, D, D, D, D, D, 264, 384)],
        dma((SENDS,)), dma((COPIES,)), dma((13,)),
    ]
    return pl.pallas_call(
        kernel,
        out_shape=pltpu.VMEM((128, D), BF16),
        in_specs=[hbm] * 13,
        out_specs=vmem,
        scratch_shapes=scratch,
        compiler_params=pltpu.CompilerParams(
            collective_id=0, has_side_effects=True, vmem_limit_bytes=62 * 1024 * 1024
        ),
    )(
        tokens_in, ln1_gain, ln1_bias, proj_bias, ln2_gain, ln2_bias, fc2_bias, qkv_bias, fc1_bias,
        qkv_weight, proj_weight, fc1_weight, fc2_weight,
    )


def solution(mesh):
    in_specs = (
        P(("row", "col"), None), P(), P(), P("row", "col"), P("col"), P("col", "row"), P(),
        P(), P(), P("row", "col"), P("col"), P("row", "col"), P(),
    )
    return jax.shard_map(
        local, mesh=mesh, in_specs=in_specs, out_specs=P(("row", "col"), None), check_vma=False
    )
```

profile of v0, /device:TPU:1, one launch (start us, length us, event | category | flops | bytes accessed | tf_op | source)
XLA Modules:
  0.0 77.1 jit_solution(14160821351597408634)
XLA Ops:
  0.0 76.4 %shard_map.127 = bf16[128,1408]{1,0:T(8,128)(2,1)S(1)} custom-call(bf16[128,1408]{1,0:T(8,128)(2,1)} %tok_in.1, bf16[1408]{0:T(1024)(128)(2,1)} %g1.1, bf16[1408]{0:T(1024)(128)(2,1)} %b1.1, bf16[1408]{0:T(1024)(128)(2,1)} %pb.1, bf16[1408]{0:T(1024)(128)(2,1)} %g2.1, bf16[1408]{0:T(1024)(128)(2,1)} %b2.1, bf16[1408]{0:T(1024)(128)(2,1)} %cb.1, ...), custom_call_target="tpu_custom_call" | custom-call | tf_op jit(solution)/shard_map/pallas_call | solution.py:539
  76.4 0.7 copy.15
where the time goes:
time: 77.2 us; the launch traced here: 77.1 us
  Pallas kernels  76.4 us (99%)
    pallas_call x1, Pallas kernels, local(): pl.pallas_call(kernel, out_shape=pltpu.VMEM((128, D), BF16), in_specs=[hb...  76.4 us

commit v1 on v0

--- a/solution.py
+++ b/solution.py
@@ -22,8 +22,8 @@
     35, 32, 30, 26, 10, 88, 11, 60, 61, 68, 12, 33, 48, 80, 67, 49, 51, 50, 64, 65, 79, 104, 71,
     103, 36, 106, 37, 98, 85, 107, 86, 97, 38, 69, 70, 105, 83, 108, 63, 109, 53, 110, 52, 113, 114,
     119, 120, 72, 95, 111, 112, 90, 123, 124, 66, 115, 116, 121, 81, 122, 117, 118, 99, 82, 94, 87,
-    76, 100, 93, 101, 92, 125, 126, 127, 84, 128, 133, 139, 130, 96, 78, 136, 102, 140, 134, 131,
-    145, 137, 141, 142, 132, 135, 138, 129, 148, 153, 152, 147, 144, 158, 163, 162, 150, 156, 143,
+    76, 100, 93, 101, 92, 125, 126, 127, 84, 128, 130, 136, 133, 139, 129, 96, 78, 102, 131, 137,
+    134, 140, 145, 141, 142, 132, 135, 138, 148, 153, 152, 147, 144, 158, 163, 162, 150, 156, 143,
     146, 160, 173, 164, 167, 170, 149, 155, 154, 159, 165, 166, 174, 175, 168, 169, 171, 172, 151,
     157, 161, 176,
 )
@@ -32,8 +32,8 @@
     7, 8, 14, 1, 3, 10, 12, 13, 15, 2, 9, 11, 23, 24, 25, 4, 26, 21, 6, 5, 18, 7, 17, 16, 20, 3, 0,
     22, 19, 8, 14, 10, 12, 1, 13, 9, 25, 7, 11, 2, 26, 17, 27, 23, 16, 24, 6, 15, 4, 12, 21, 1, 0,
     18, 8, 19, 14, 3, 5, 10, 9, 20, 25, 16, 24, 17, 11, 13, 26, 21, 22, 23, 4, 12, 27, 2, 7, 6, 0,
-    18, 15, 1, 19, 14, 8, 25, 3, 5, 10, 24, 16, 17, 20, 11, 26, 13, 9, 22, 23, 4, 21, 0, 12, 27, 7,
-    18, 2, 15, 1, 6, 8, 19, 25, 14, 10, 5, 16, 11,
+    18, 15, 1, 19, 14, 8, 25, 3, 5, 10, 24, 16, 17, 20, 11, 26, 13, 9, 22, 23, 4, 21, 0, 12, 27, 8,
+    7, 18, 2, 15, 1, 6, 3, 19, 14, 25, 10, 24, 20,
 )
 SCALE = (1.0 / HEAD**0.5) * 1.4426950408889634
 NT = (((1,), (1,)), ((), ()))

time: 77.2 us -> 77 us (level)
  no operation moved by 1% of the time
where the time goes in v1:
time: 77 us; the launch traced here: 76.9 us
  Pallas kernels  76.2 us (99%)
    pallas_call x1, Pallas kernels, local(): pl.pallas_call(kernel, out_shape=pltpu.VMEM((128, D), BF16), in_specs=[hb...  76.2 us

profile of v1, /device:TPU:1, one launch (start us, length us, event | category | flops | bytes accessed | tf_op | source)
XLA Modules:
  0.0 76.9 jit_solution(8564942987326106932)
XLA Ops:
  0.0 76.2 %shard_map.127 = bf16[128,1408]{1,0:T(8,128)(2,1)S(1)} custom-call(bf16[128,1408]{1,0:T(8,128)(2,1)} %tok_in.1, bf16[1408]{0:T(1024)(128)(2,1)} %g1.1, bf16[1408]{0:T(1024)(128)(2,1)} %b1.1, bf16[1408]{0:T(1024)(128)(2,1)} %pb.1, bf16[1408]{0:T(1024)(128)(2,1)} %g2.1, bf16[1408]{0:T(1024)(128)(2,1)} %b2.1, bf16[1408]{0:T(1024)(128)(2,1)} %cb.1, ...), custom_call_target="tpu_custom_call" | custom-call | tf_op jit(solution)/shard_map/pallas_call | solution.py:539
  76.2 0.7 copy.15
